TPU v7x, 512 devices: a whole 4x4x16 slice. The times are simulated.
512 devices in a mesh: tm: 64 (over y, z), chan: 8 (over x, core).
Axes of the slice: x: 4, y: 4, z: 16, core: 2. Of those that a mesh axis runs over, the one named last changes fastest.
Arguments:
- data: bfloat16 [6144, 8192], P('chan', 'tm'), may hold values from -6 to 6
- basis: float32 [6, 61], replicated, may hold values from -0.75 to 0.75
- templates: float32 [2048, 192], P(('tm', 'chan')), may hold values from -18 to 18
- spike_offset: int32 [2048], P('tm'), may hold values from 0 to 127, as said below
- spike_unit: int32 [2048], P('tm'), may hold values from 0 to 2047, as said below
- spike_amp: float32 [2048], P('tm'), may hold values from 0.5 to 2
- seg_count: int32 [64], P('tm'), may hold values from 16 to 32
- neighbors: int32 [2048, 32], replicated, may hold values from 0 to 6143, as said below
Outputs:
- residual: bfloat16 [6144, 8192], P('chan', 'tm')
- new_templates: float32 [2048, 192], P(('tm', 'chan'))
Inputs may be any that keep to these rules, and one draw needn't show every extreme that they name: `spike_offset`: in every segment slot i < 8 has an offset below 30, slot i with 8 <= i < 16 an offset of 98 or more. `spike_unit`: in every segment slot i < 16 names a unit of the (i mod 8)-th of 8 equal bands of unit numbers. `neighbors`: row k holds 32 consecutive channels, rising, whose first differs by at most 16 from floor(k * 6112 / 2047).
All inputs are finite; a program needn't handle non-finite values.
Results may differ from a plain program's by a relative error of at most 0.0034.
Values may be sent and summed in bfloat16 or wider, within the bound.
A program may use at most 64 MiB of HBM per device.

v0:
```python
import math

import jax
import jax.numpy as jnp
from jax import lax
from jax.sharding import PartitionSpec as P

prior_weight = 4.0


def extended(x, sides, width):
    for axis, dim in sides:
        size, length = (lax.axis_size(axis), x.shape[dim])
        up = [(i, (i + 1) % size) for i in range(size - 1)]
        down = [(j, i) for i, j in up]
        last = lax.slice_in_dim(x, length - width, length, axis=dim)
        leading = lax.slice_in_dim(x, 0, width, axis=dim)
        before = lax.ppermute(last, axis, up)
        after = lax.ppermute(leading, axis, down)
        x = jnp.concatenate([before, x, after], axis=dim)
    return x


def shifted_basis(basis_low, offsets, width):
    columns = jnp.arange(width, dtype=jnp.int32)
    lag_index = columns[None, :] - offsets[:, None]
    tap_count = basis_low.shape[1]
    inside = (lag_index >= 0) & (lag_index < tap_count)
    picked = jnp.take(basis_low, jnp.clip(lag_index, 0, tap_count - 1), axis=1)
    return jnp.where(inside[None, :, :], picked, jnp.zeros((), basis_low.dtype))


def channel_hits(chan_rows, group_start, group_width):
    local_chan = chan_rows - group_start
    return (
        local_chan[:, :, None] == jnp.arange(group_width, dtype=jnp.int32)[None, None, :]
    ).astype(jnp.bfloat16)


def render_block(coef_low, chan_hits, shifted):
    placed = jnp.einsum(
        "sbj,sjc->bsc", coef_low, chan_hits, preferred_element_type=jnp.float32
    ).astype(jnp.bfloat16)
    return jnp.einsum("bsc,bsw->cw", placed, shifted, preferred_element_type=jnp.float32)


def extract_block(res_ext, chan_hits, shifted):
    along = jnp.einsum("cw,bsw->bsc", res_ext, shifted, preferred_element_type=jnp.float32)
    return jnp.einsum(
        "bsc,sjc->sbj", along, chan_hits.astype(jnp.float32), precision=lax.Precision.HIGHEST
    )


def shards(data, basis, templates, spike_offset, spike_unit, spike_amp, seg_count, neighbors):
    group_width, seg_len = data.shape
    slot_count = spike_offset.shape[0]
    basis_count, tap_count = basis.shape
    half_width = (tap_count - 1) // 2
    ext_len = seg_len + 2 * half_width
    nbr_width = neighbors.shape[1]
    group_start = lax.axis_index("chan") * group_width
    basis_low = basis.astype(jnp.bfloat16)
    basis_gram = jnp.dot(basis, basis.T, precision=lax.Precision.HIGHEST)
    live_mask = jnp.arange(slot_count, dtype=jnp.int32) < seg_count[0]
    weight = jnp.where(live_mask, spike_amp, jnp.zeros((), jnp.float32))
    all_coef = lax.all_gather(templates, ("tm", "chan"), axis=0, tiled=True)
    unit_count = all_coef.shape[0]
    spike_coef = jnp.take(all_coef, spike_unit, axis=0).reshape(slot_count, basis_count, nbr_width)
    spike_chans = jnp.take(neighbors, spike_unit, axis=0)
    block_rows = math.gcd(slot_count, 32)
    used_blocks = (seg_count[0] + block_rows - 1) // block_rows

    def block_parts():
        chan_hits = channel_hits(spike_chans, group_start, group_width)
        shifted = shifted_basis(basis_low, spike_offset, ext_len)
        return (spike_coef, weight, live_mask, chan_hits, shifted)

    def add_block(block_index, model_sum):
        coef_rows, amp_rows, live_rows, chan_hits, shifted = block_parts()
        coef_low = (amp_rows[:, None, None] * coef_rows).astype(jnp.bfloat16)
        return model_sum + render_block(coef_low, chan_hits, shifted)

    model_sum = lax.fori_loop(
        0, used_blocks, add_block, jnp.zeros((group_width, ext_len), jnp.float32)
    )
    spill_cols = jnp.concatenate(
        [model_sum[:, :half_width], model_sum[:, seg_len + half_width :]], axis=1
    )
    incoming = extended(spill_cols, (("tm", 1),), half_width)
    centre_model = model_sum[:, half_width : seg_len + half_width]
    centre_model = centre_model.at[:, :half_width].add(incoming[:, :half_width])
    centre_model = centre_model.at[:, seg_len - half_width :].add(incoming[:, 3 * half_width :])
    residual = (data.astype(jnp.float32) - centre_model).astype(jnp.bfloat16)
    res_ext = extended(residual, (("tm", 1),), half_width)

    def feature_block(block_index, features):
        coef_rows, amp_rows, live_rows, chan_hits, shifted = block_parts()
        projected = extract_block(res_ext, chan_hits, shifted)
        own_term = amp_rows[:, None, None] * jnp.einsum(
            "bk,skj->sbj", basis_gram, coef_rows, precision=lax.Precision.HIGHEST
        )
        in_group = jnp.sum(chan_hits.astype(jnp.float32), axis=2)
        combined = projected + own_term * in_group[:, None, :]
        combined = jnp.where(live_rows[:, None, None], combined, jnp.zeros((), jnp.float32))
        return combined.reshape(block_rows, basis_count * nbr_width)

    features = lax.fori_loop(
        0, used_blocks, feature_block, jnp.zeros((slot_count, basis_count * nbr_width), jnp.float32)
    )
    unit_pick = (spike_unit[:, None] == jnp.arange(unit_count, dtype=jnp.int32)[None, :]).astype(
        jnp.float32
    )
    unit_pick = unit_pick * live_mask.astype(jnp.float32)[:, None]
    unit_sums = jnp.einsum("su,sk->uk", unit_pick, features, precision=lax.Precision.HIGHEST)
    spike_tally = jnp.sum(unit_pick, axis=0)
    owner_count = lax.axis_size("tm") * lax.axis_size("chan")
    per_owner = unit_count // owner_count
    first_group = (lax.axis_index("chan") == 0).astype(jnp.float32)
    counts = spike_tally * first_group
    total_sums, total_counts = lax.psum((unit_sums, counts), ("tm", "chan"))
    owner_index = lax.axis_index("tm") * lax.axis_size("chan") + lax.axis_index("chan")
    mine_sums = lax.dynamic_slice_in_dim(total_sums, owner_index * per_owner, per_owner)
    mine_counts = lax.dynamic_slice_in_dim(total_counts, owner_index * per_owner, per_owner)
    updated = (prior_weight * templates + mine_sums) / (prior_weight + mine_counts[:, None])
    return (residual, updated)


def solution(mesh):
    return jax.shard_map(
        shards,
        mesh=mesh,
        in_specs=(
            P("chan", "tm"),
            P(),
            P(("tm", "chan"), None),
            P("tm"),
            P("tm"),
            P("tm"),
            P("tm"),
            P(),
        ),
        out_specs=(P("chan", "tm"), P(("tm", "chan"), None)),
        check_vma=False,
    )
```

profile of v0, /device:TPU:1, one launch (start us, length us, event | category | flops | bytes accessed | tf_op | source)
XLA Modules:
  0.0 746.6 jit_solution(11560176758011798824)
XLA Ops:
  7.2 0.7 all-gather.3.cloned.1.call-update
  8.6 0.8 copy.38
  9.4 0.7 compare_select_fusion.1
  10.3 1.1 copy.36
  11.4 1.3 copy.37
  12.7 11.9 %gather_fusion.3 = bf16[6016,6]{1,0:T(8,128)(2,1)S(1)} fusion(bf16[6,61]{0,1:T(8,128)(2,1)S(1)} %copy.38, s32[6144]{0:T(1024)S(1)} %pad_clamp_fusion.1), kind=kCustom, calls=%fused_computation.1.clone | custom fusion | bytes 168448 | tf_op jit(solution)/shard_map/while/body/jit(_take)/gather | solution.py:29
  24.6 1.3 copy.39
  26.9 0.7 compare_reduce_fusion
  28.5 185.6 %all-gather.3.cloned.1.call-done = f32[512,4,192]{2,1,0:T(4,128)} async-done(((f32[1,4,192]{2,1,0:T(4,128)}), f32[512,4,192]{2,1,0:T(4,128)}) %all-gather.3.cloned.1.call-update) | async-done | bytes 1572880 | tf_op jit(solution)/shard_map/all_gather | solution.py:66
  214.1 2.0 reshape.185
  216.9 14.9 %while.26 = (s32[]{:T(128)}, f32[768,188]{0,1:T(8,128)S(1)}, s32[]{:T(128)}, s32[]{:T(128)}, s32[32,32]{1,0:T(8,128)S(1)}, /*index=5*/f32[32]{0:T(128)S(1)}, f32...) while((s32[]{:T(128)}, f32[768,188]{0,1:T(8,128)S(1)}, s32[]{:T(128)}, ...), condition=%wide.region_1.3_spmd, body=%wide.region_0.2_spmd.sunk | while | flops 66146816 | bytes 2456553 | solution.py:83
  217.3 0.6 fusion.60
  217.9 11.9 %gather_fusion = bf16[6016,6]{1,0:T(8,128)(2,1)S(1)} fusion(bf16[6,61]{0,1:T(8,128)(2,1)S(1)} %get-tuple-element.462, s32[6144]{0:T(1024)S(1)} %pad_clamp_fusion.4), kind=kCustom, calls=%fused_computation.clone.clone.1 | custom fusion | bytes 168448 | tf_op jit(solution)/shard_map/while/body/jit(_take)/gather | solution.py:29
  229.8 1.3 copy.49
  231.9 3.2 collective-permute-start
  235.1 1.3 collective-permute-start.1
  236.9 0.7 add_select_fusion
  237.6 0.8 scatter-add.6
  238.4 2.4 collective-permute-done.1
  241.4 2.1 collective-permute-start.2
  243.5 1.3 collective-permute-start.3
  245.0 3.3 collective-permute-done.3
  248.6 1.8 fusion.20
  250.4 0.6 broadcast_in_dim.113
  251.0 1.5 while.27
  251.0 0.6 iota_compare_fusion.14
  251.8 0.7 reshape.207
  252.5 4.0 fusion.24
  256.6 107.3 %psum.15 = f32[2048]{0:T(1024)S(1)} all-reduce(f32[2048]{0:T(1024)S(1)} %broadcast_multiply_fusion), channel_id=1, replica_groups=mesh['tm'=64,'chan'=8] {'tm','chan'}, use_global_device_ids=true, to_apply=%region_8.10 | all-reduce | flops 2048 | bytes 16384 | tf_op jit(solution)/shard_map/psum | solution.py:120
  364.0 0.8 copy.41
  364.8 373.6 %all-reduce.2.cloned.1.call-done = f32[2048,192]{1,0:T(8,128)} async-done(((f32[2048,192]{1,0:T(8,128)}), f32[2048,192]{1,0:T(8,128)}) %all-reduce.2.cloned.1.call-update) | async-done | bytes 1572880 | tf_op jit(solution)/shard_map/psum | solution.py:120
  738.4 1.4 add_divide_fusion
  (51 shorter events, 5.7 us)
Async XLA Ops:
  7.2 206.9 %all-gather.3.cloned.1.call-start = ((), (), s32[]{:S(2)}) async-start(), calls=%async_computation.1 | async-start | bytes 2101248 | tf_op jit(solution)/shard_map/all_gather | solution.py:66
  7.9 730.5 %all-reduce.2.cloned.1.call-start = ((), (), s32[]{:S(2)}) async-start(), calls=%async_computation | async-start | bytes 4194304 | tf_op jit(solution)/shard_map/psum | solution.py:120
  11.4 14.9 %copy-start.3 = (s32[32]{0:T(128)S(1)}, s32[32]{0:T(128)}, u32[]{:S(2)}) copy-start(s32[32]{0:T(128)} %param.22) | copy-start | bytes 388
  11.4 16.2 %copy-start.1 = (f32[6,61]{1,0:T(8,128)S(1)}, f32[6,61]{1,0:T(8,128)}, u32[]{:S(2)}) copy-start(f32[6,61]{1,0:T(8,128)} %param.19) | copy-start | bytes 4396
  11.4 17.0 %copy-start.4 = (f32[32]{0:T(128)S(1)}, f32[32]{0:T(128)}, u32[]{:S(2)}) copy-start(f32[32]{0:T(128)} %param.23) | copy-start | bytes 388
  11.4 17.0 %copy-start = (s32[32]{0:T(128)S(1)}, s32[32]{0:T(128)}, u32[]{:S(2)}) copy-start(s32[32]{0:T(128)} %param.21) | copy-start | bytes 388
  231.9 5.1 collective-permute-start
  235.1 5.7 collective-permute-start.1
  241.4 3.6 collective-permute-start.2
  243.5 4.8 collective-permute-start.3
  252.5 485.9 %copy-start.2 = (f32[4,192]{1,0:T(4,128)S(1)}, f32[4,192]{1,0:T(4,128)}, u32[]{:S(2)}) copy-start(f32[4,192]{1,0:T(4,128)} %param.20) | copy-start | bytes 9220
Sparse Core Ops, SparseCore 0:
  12.6 201.4 all-gather.2
  256.6 481.7 all-reduce.1
where the time goes:
time: 747 us
  waiting for transfers between devices  566 us (76%)
  blocking collectives  107 us (14%)
  local copies, waits for them, and re-layouts  37.2 us (5%)
  between operations  15.1 us (2%)
  starting transfers between devices  7.97 us (1%)
    psum x1, waiting for transfers between devices, shards(): total_sums, total_counts = lax.psum((unit_sums, counts), ('tm', 'chan'))  374 us
    all_gather x1, waiting for transfers between devices, shards(): all_coef = lax.all_gather(templates, ('tm', 'chan'), axis=0, tiled=True)  186 us
    psum x1, blocking collectives, shards(): total_sums, total_counts = lax.psum((unit_sums, counts), ('tm', 'chan'))  107 us
    gather x6, local copies, waits for them, and re-layouts, shifted_basis(): picked = jnp.take(basis_low, jnp.clip(lag_index, 0, tap_count - 1), axis=1)  27 us
  transfers between devices with their start and end apart: 6, of which 5 were waited for; matrix products, arithmetic and copies ran while one was open for 3% of the time, Pallas kernels for 0%

commit v1 on v0

v1 whole, which is shorter than its diff:
```python
import functools

import jax
import jax.numpy as jnp
from jax import lax
from jax.experimental import pallas as pl
from jax.experimental.pallas import tpu as pltpu
from jax.sharding import PartitionSpec as P

MESH = pl.DeviceIdType.MESH
HI = lax.Precision.HIGHEST
BF = jnp.bfloat16
F32 = jnp.float32
I32 = jnp.int32
prior_weight = 4.0
LANES = 128
PER = 4
NBR = 32


def iota(shape, dim):
    return lax.broadcasted_iota(I32, shape, dim)


def dot(a, b, dims=((1,), (0,)), precision=None):
    return lax.dot_general(a, b, (dims, ((), ())), precision=precision, preferred_element_type=F32)


def one(mask, dtype=F32):
    return jnp.where(mask, 1.0, 0.0).astype(dtype)


def kernel(
    nt, nz, nc, group, taps,
    data, basis, templ, off, unit, amp, count, nbr,
    res_out, new_out,
    nbx, nbo, bp, mrow, msend, mrecv, hsend, hrecv, asrc, abuf, toep, shifted, maskc, placed, res,
    tbuf, ubuf, cbuf, csrc, dbuf,
    nsem, msem_s, msem_r, hsem_s, hsem_r, a1s, a1r, a2s, a2r, c1s, c1r, c2s, c2r,
):
    ny = nt // nz
    rb = nt // nc
    nrow = rb + 2
    row_units = nc * PER
    nb = basis.shape[0]
    half = (taps - 1) // 2
    quarter = group // 4
    shards = nrow * nc
    width = nb * LANES
    hw = width // 2
    t = lax.axis_index("tm")
    c = lax.axis_index("chan")
    y = t // nz
    z = t % nz
    band = t // rb
    at_low = (t % rb) == 0
    at_high = (t % rb) == rb - 1
    edge = jnp.logical_or(at_low, at_high)
    edge_band = jnp.where(at_low, (band + nc - 1) % nc, (band + 1) % nc)
    rr = (z + 2 * nz - (rb * c - 1) % nz) % nz
    gathers = rr < nrow
    src_row = (rb * c + nt - 1 + rr) % nt
    right = (t + 1) % nt
    left = (t + nt - 1) % nt

    barrier = pltpu.get_barrier_semaphore()

    def greet(tm, chan):
        pl.semaphore_signal(barrier, inc=1, device_id=(tm, chan), device_id_type=MESH)

    for d in range(1, nz):
        greet(y * nz + (z + d) % nz, c)
    greet(right, c)
    greet(left, c)
    n_greet = nz - 1 + 2 + jnp.where(edge, 2 * ny, ny) + jnp.where(gathers, nc, 0)
    own_main = band == c
    own_edge = jnp.logical_and(edge, edge_band == c)
    n_greet = n_greet - jnp.where(jnp.logical_or(own_main, own_edge), 1, 0)
    n_greet = n_greet - jnp.where(jnp.logical_and(gathers, src_row == t), 1, 0)
    for yy in range(ny):
        @pl.when(jnp.logical_or(yy != y, band != c))
        def _():
            greet(yy * nz + z, band)

        @pl.when(jnp.logical_and(edge, jnp.logical_or(yy != y, edge_band != c)))
        def _():
            greet(yy * nz + z, edge_band)
    for ch in range(nc):
        @pl.when(jnp.logical_and(gathers, jnp.logical_or(src_row != t, ch != c)))
        def _():
            greet(src_row, ch)

    lowest = (rb * c + nt - 1) % nt
    highest = (rb * c + rb) % nt
    copies = [
        pltpu.make_async_copy(nbr.at[pl.ds(lowest * row_units, row_units)], nbx.at[pl.ds(0, row_units)], nsem.at[0]),
        pltpu.make_async_copy(
            nbr.at[pl.ds(c * rb * row_units, rb * row_units)], nbx.at[pl.ds(row_units, rb * row_units)], nsem.at[1]
        ),
        pltpu.make_async_copy(
            nbr.at[pl.ds(highest * row_units, row_units)],
            nbx.at[pl.ds((rb + 1) * row_units, row_units)],
            nsem.at[2],
        ),
        pltpu.make_async_copy(nbr.at[pl.ds(t * row_units, row_units)], nbo, nsem.at[3]),
    ]
    for cp in copies:
        cp.start()

    mrow[...] = jnp.zeros_like(mrow)
    slots = off.shape[1]
    live = (iota((1, slots), 1) < count[...]).astype(F32)
    mrow[0:1, 0:slots] = unit[...].astype(F32)
    mrow[1:2, 0:slots] = off[...].astype(F32)
    mrow[2:3, 0:slots] = jnp.where(live > 0.0, amp[...], 0.0)
    mrow[3:4, 0:slots] = live
    meta = mrow[...]
    lane8 = iota((8, LANES), 1)
    row8 = iota((8, LANES), 0)
    go_right = jnp.where(t == nt - 1, 0.0, 1.0)
    go_left = jnp.where(t == 0, 0.0, 1.0)
    seg = data.shape[1]
    to_right = jnp.where(row8 == 1, meta - float(seg), jnp.where(row8 >= 2, meta * go_right, meta))
    to_left = jnp.where(row8 == 1, meta + float(seg), jnp.where(row8 >= 2, meta * go_left, meta))
    to_right = jnp.where(lane8 < slots, to_right, 0.0)
    to_left = jnp.where(lane8 < slots, to_left, 0.0)
    msend[0] = pltpu.roll(to_right, slots, 1)
    msend[1] = pltpu.roll(to_left, 2 * slots, 1)

    sel_i = iota((seg, 2 * LANES), 0)
    sel_j = iota((seg, 2 * LANES), 1)
    pack = jnp.zeros((quarter, 2 * LANES), F32)
    for k in range(4):
        to_r = (sel_j == sel_i - (seg - 32) + 32 * k) & (sel_i >= seg - 32)
        to_l = (sel_j == sel_i + 32 * k + LANES) & (sel_i < 32)
        pack = pack + dot(data[k * quarter:(k + 1) * quarter, :], one(to_r | to_l, BF))
    hsend[0] = pack[:, :LANES].astype(BF)
    hsend[1] = pack[:, LANES:].astype(BF)

    copies[3].wait()
    starts_own = nbo[:, 0:1]
    pick = iota((row_units, LANES), 0) == PER * c + iota((row_units, LANES), 1) // NBR
    s_lane = jnp.sum(jnp.where(pick, starts_own, 0), axis=0, keepdims=True)
    coef = nb * NBR
    turn = one(((iota((coef, LANES), 0) + s_lane - iota((coef, LANES), 1)) & (NBR - 1)) == 0)
    q_of = iota((8, coef), 1) // NBR
    b_of = iota((8, coef), 0)
    spread = jnp.concatenate([jnp.where(q_of == b_of, templ[u:u + 1, :], 0.0) for u in range(PER)], axis=0)
    turned = dot(spread, turn, precision=HI)
    lane_u = iota((8, LANES), 1) // NBR
    tblk = jnp.zeros((8, LANES), F32)
    for u in range(PER):
        tblk = tblk + jnp.where(lane_u == u, turned[8 * u:8 * u + 8, :], 0.0)
    asrc[...] = tblk

    pl.semaphore_wait(barrier, n_greet)

    def remote(src, dst, s, r, tm, chan):
        return pltpu.make_async_remote_copy(
            src_ref=src, dst_ref=dst, send_sem=s, recv_sem=r, device_id=(tm, chan), device_id_type=MESH
        )

    def block8(ref, i):
        return ref.at[pl.ds(pl.multiple_of(8 * i, 8), 8), :]

    def a1_copy(yy, e):
        return remote(asrc, block8(abuf, c), a1s.at[e * ny + yy], a1r.at[c], yy * nz + z, edge_band if e else band)

    for yy in range(ny):
        @pl.when(jnp.logical_or(yy != y, band != c))
        def _():
            a1_copy(yy, 0).start()

        @pl.when(jnp.logical_and(edge, jnp.logical_or(yy != y, edge_band != c)))
        def _():
            a1_copy(yy, 1).start()

    @pl.when(jnp.logical_or(own_main, own_edge))
    def _():
        block8(abuf, c)[...] = asrc[...]

    m_right = remote(msend.at[0], mrecv.at[0], msem_s.at[0], msem_r.at[0], right, c)
    m_left = remote(msend.at[1], mrecv.at[1], msem_s.at[1], msem_r.at[1], left, c)
    h_right = remote(hsend.at[0], hrecv.at[0], hsem_s.at[0], hsem_r.at[0], right, c)
    h_left = remote(hsend.at[1], hrecv.at[1], hsem_s.at[1], hsem_r.at[1], left, c)
    m_right.start()
    m_left.start()
    h_right.start()
    h_left.start()

    bp[...] = jnp.zeros_like(bp)
    bp[0:nb, 0:taps] = basis[...]
    span = 2 * LANES
    base = 66
    lane_s = iota((LANES, LANES), 1)

    def shifts(b):
        row = jnp.broadcast_to(bp[b:b + 1, :].astype(BF).astype(F32), (LANES, span))
        for r0 in (0, LANES):
            mid = pltpu.roll(row, (span - half - base + r0) % span, 1, stride=1, stride_axis=0)[:, :LANES]
            low = pltpu.roll(row, (span - half - base + 32 + r0) % span, 1, stride=1, stride_axis=0)[:, :LANES]
            high = pltpu.roll(row, (span - half - base - seg + 32 + r0) % span, 1, stride=1, stride_axis=0)[:, :LANES]
            side = jnp.where(lane_s < 32, low, jnp.where(lane_s < 64, high, 0.0))
            toep[b, r0:r0 + LANES, 0:LANES] = mid.astype(BF)
            toep[b, r0:r0 + LANES, LANES:span] = side.astype(BF)

    for b in range(nb):
        shifts(b)
    gram = dot(bp[...], bp[...], ((1,), (1,)), precision=HI)
    gram_t = dot(gram, tblk, precision=HI)

    @pl.when(gathers)
    def _():
        for ch in range(nc):
            @pl.when(jnp.logical_or(src_row != t, ch != c))
            def _():
                remote(asrc, block8(abuf, ch), a1s.at[0], a1r.at[ch], src_row, ch).wait_recv()
        rows = [abuf[pl.ds(b, nc, stride=8), :] for b in range(nb)]
        top = jnp.concatenate(rows[: nb // 2], axis=1)
        bottom = jnp.concatenate(rows[nb // 2:], axis=1)
        tbuf[rr] = jnp.concatenate([top, bottom], axis=0).astype(BF)
        for d in [nz // 2] + [s * k for k in range(nz // 2 - 1, 0, -1) for s in (1, -1)]:
            remote(tbuf.at[rr], tbuf.at[rr], a2s.at[d % nz], a2r.at[rr], y * nz + (z + d + nz) % nz, c).start()

    m_right.wait_recv()
    m_left.wait_recv()
    every = meta + mrecv[0] + mrecv[1]
    for cp in copies[:3]:
        cp.wait()
    units_x = nrow * row_units
    unit_lane = every[0:1, :].astype(I32)
    found = (iota((units_x, LANES), 0) + row_units * (rb * c - 1)) == unit_lane
    start_lane = jnp.sum(jnp.where(found, nbx[:, 0:1], 0), axis=0, keepdims=True) - group * c
    shard_lane = unit_lane // PER - nc * (rb * c - 1)
    sub_lane = unit_lane % PER
    live_lane = every[3:4, :]
    amp_lane = every[2:3, :]
    stack = jnp.where(row8 == 0, every[1:2, :] + float(base), 0.0)
    stack = jnp.where(row8 == 1, shard_lane.astype(F32), stack)
    stack = jnp.where(row8 == 2, sub_lane.astype(F32), stack)
    stack = jnp.where(row8 == 3, amp_lane, stack)
    stack = jnp.where(row8 == 4, start_lane.astype(F32), stack)
    cols = jnp.transpose(stack)
    pos_col = cols[:, 0:1].astype(I32)
    shard_col = cols[:, 1:2].astype(I32)
    sub_col = cols[:, 2:3].astype(I32)
    amp_col = cols[:, 3:4]
    start_col = cols[0:slots, 4:5].astype(I32)

    at_pos = one(pos_col == iota((LANES, span), 1), BF)
    for b in range(nb):
        shifted[b * LANES:(b + 1) * LANES, :] = dot(at_pos, toep[b]).astype(BF)
    maskc[...] = one(
        (iota((group, LANES), 0) >= start_lane) & (iota((group, LANES), 0) < start_lane + NBR), BF
    )
    own_mask = one((iota((slots, group), 1) >= start_col) & (iota((slots, group), 1) < start_col + NBR))
    shard_n = one(shard_col == iota((LANES, shards), 1), BF)
    n_shard = one(shard_lane == iota((shards, LANES), 0)) * live_lane
    lane_sub = iota((LANES, LANES), 1) // NBR
    weigh = jnp.where(lane_sub == sub_col, amp_col, 0.0)
    fold = one((iota((NBR, LANES), 1) & (NBR - 1)) == iota((NBR, LANES), 0), BF)
    spin = one((iota((LANES, LANES), 1) & (NBR - 1)) == (iota((LANES, LANES), 0) & (NBR - 1)), BF)
    sub_own = one(lane_sub == sub_col)[0:slots, :]

    l_i = iota((LANES, LANES), 1)
    tally_w = jnp.where(l_i < PER, one(l_i == sub_col), 0.0)
    tally_w = tally_w + jnp.where((l_i >= PER) & (l_i < 3 * PER), one((l_i & (PER - 1)) == sub_col) * amp_col, 0.0)
    tally_w = jnp.where(iota((LANES, LANES), 0) < slots, tally_w, 0.0)
    tally = dot(n_shard, tally_w, precision=HI)
    t_i = iota((shards, LANES), 0)
    tally = jnp.where((t_i >= nc) & (t_i < nc * (rb + 1)), tally, 0.0)
    coarse = tally.astype(BF).astype(F32)
    tally = jnp.where(iota((shards, LANES), 1) < 2 * PER, coarse, tally - coarse)

    h_right.wait_recv()
    h_left.wait_recv()
    un_i = iota((LANES, LANES), 0)
    un_j = iota((LANES, LANES), 1)
    wings = []
    for k in range(4):
        from_l = one((un_i == un_j + 32 * k) & (un_j < 32), BF)
        from_r = one((un_i == un_j - 32 + 32 * k) & (un_j >= 32) & (un_j < 64), BF)
        wings.append(dot(hrecv[0], from_l) + dot(hrecv[1], from_r))
    wing = jnp.concatenate(wings, axis=0)
    wing_lane = iota((group, LANES), 1)
    inside = ((wing_lane < 32) & (t > 0)) | ((wing_lane >= 32) & (wing_lane < 64) & (t < nt - 1))

    for k in range(nrow):
        zk = (rb * c + 2 * nz - 1 + k) % nz

        @pl.when(zk != z)
        def _():
            remote(tbuf.at[k], tbuf.at[k], a2s.at[0], a2r.at[k], y * nz + zk, c).wait_recv()
    blocks = [tbuf[k].astype(F32) for k in range(nrow)]
    t_top = jnp.concatenate([v[:nc] for v in blocks], axis=0).astype(BF)
    t_bottom = jnp.concatenate([v[nc:] for v in blocks], axis=0).astype(BF)
    chosen = [dot(shard_n, t_top), dot(shard_n, t_bottom)]
    for b in range(nb):
        part = chosen[b // (nb // 2)]
        b3 = b % (nb // 2)
        low = (part[:, b3 * LANES:(b3 + 1) * LANES] * weigh).astype(BF)
        lowt = dot(fold, low, ((1,), (1,))).astype(BF)
        placed[:, b * LANES:(b + 1) * LANES] = jnp.concatenate([lowt] * (group // NBR), axis=0) * maskc[...]
    model = dot(placed[...], shifted[...])
    centre = (data[...].astype(F32) - model[:, :LANES]).astype(BF)
    res_out[...] = centre
    res[:, 0:LANES] = centre
    res[:, LANES:span] = jnp.where(inside, wing - model[:, LANES:], 0.0).astype(BF)

    own_shift = jnp.concatenate([shifted[b * LANES:b * LANES + slots, :] for b in range(nb)], axis=0)
    along = dot(own_shift, res[...], ((1,), (1,)))
    own_all = jnp.concatenate([own_mask] * nb, axis=0)
    hit = along * own_all
    feat = hit[:, 0:LANES]
    for k in range(1, group // LANES):
        feat = feat + hit[:, k * LANES:(k + 1) * LANES]
    feat = dot(feat.astype(BF), spin)
    spread_w = jnp.concatenate([feat[b * slots:(b + 1) * slots, :] * sub_own for b in range(nb)], axis=1)
    sums = dot(n_shard[:, 0:slots].astype(BF), spread_w.astype(BF))
    for k in range(nrow):
        lo, hi = k * nc, (k + 1) * nc
        top = jnp.concatenate([sums[lo:hi, :hw], tally[lo:hi, :]], axis=1)
        bottom = jnp.concatenate([sums[lo:hi, hw:], jnp.zeros((nc, LANES), F32)], axis=1)
        ubuf[k] = jnp.concatenate([top, bottom], axis=0).astype(BF)
    for k in range(nrow):
        zk = (rb * c + 2 * nz - 1 + k) % nz

        @pl.when(zk != z)
        def _():
            remote(ubuf.at[k], cbuf.at[z], c1s.at[k], c1r.at[z], y * nz + zk, c).start()

        @pl.when(zk == z)
        def _():
            cbuf[z] = ubuf[k]

    to_edge = jnp.logical_or(rr == 0, rr == nrow - 1)
    slot_out = jnp.where(to_edge, ny, 0) + y

    def c2_copy(ch):
        return remote(block8(csrc, ch), block8(dbuf, slot_out), c2s.at[ch], c2r.at[slot_out], src_row, ch)

    @pl.when(jnp.logical_not(edge))
    def _():
        dbuf[8 * ny:16 * ny, :] = jnp.zeros((8 * ny, LANES), F32)

    @pl.when(gathers)
    def _():
        for d in range(1, nz):
            zd = (z + d) % nz
            remote(ubuf.at[0], cbuf.at[zd], c1s.at[0], c1r.at[zd], y * nz + zd, c).wait_recv()
        total = cbuf[0].astype(F32)
        for k in range(1, nz):
            total = total + cbuf[k].astype(F32)
        for b in range(nb):
            r0 = nc * (b // (nb // 2))
            l0 = LANES * (b % (nb // 2))
            csrc[pl.ds(b, nc, stride=8), :] = total[r0:r0 + nc, l0:l0 + LANES]
        csrc[pl.ds(nb, nc, stride=8), :] = total[:nc, hw:]
        csrc[pl.ds(nb + 1, nc, stride=8), :] = jnp.zeros((nc, LANES), F32)
        for ch in range(nc):
            mine = jnp.logical_and(src_row == t, ch == c)

            @pl.when(jnp.logical_not(mine))
            def _():
                c2_copy(ch).start()

            @pl.when(mine)
            def _():
                block8(dbuf, slot_out)[...] = csrc[8 * ch:8 * ch + 8, :]

    for yy in range(ny):
        @pl.when(jnp.logical_or(yy != y, band != c))
        def _():
            remote(block8(csrc, 0), block8(dbuf, yy), c2s.at[0], c2r.at[yy], yy * nz + z, band).wait_recv()

        @pl.when(jnp.logical_and(edge, jnp.logical_or(yy != y, edge_band != c)))
        def _():
            remote(
                block8(csrc, 0), block8(dbuf, ny + yy), c2s.at[0], c2r.at[ny + yy], yy * nz + z, edge_band
            ).wait_recv()
    got = dbuf[0:8, :]
    for k in range(1, 2 * ny):
        got = got + dbuf[8 * k:8 * k + 8, :]
    ex_i = iota((LANES, 2 * LANES), 0)
    ex_j = iota((LANES, 2 * LANES), 1)
    ex_u = (ex_j & (LANES - 1)) // NBR
    expand = one(((ex_j < LANES) & (ex_i == ex_u)) | ((ex_j >= LANES) & ((ex_i == ex_u + PER) | (ex_i == ex_u + 2 * PER))))
    wide = dot(got, expand, precision=HI)[nb:nb + 1, :]
    fresh = (prior_weight * tblk + got + wide[:, LANES:] * gram_t) / (prior_weight + wide[:, :LANES])
    split = jnp.concatenate([jnp.where(lane_u == u, fresh, 0.0) for u in range(PER)], axis=0)
    back = dot(split, turn, ((1,), (1,)), precision=HI)
    for u in range(PER):
        piece = jnp.where(q_of == b_of, back[8 * u:8 * u + 8, :], 0.0)
        new_out[u:u + 1, :] = jnp.sum(piece, axis=0, keepdims=True)

    for yy in range(ny):
        @pl.when(jnp.logical_or(yy != y, band != c))
        def _():
            a1_copy(yy, 0).wait_send()

        @pl.when(jnp.logical_and(edge, jnp.logical_or(yy != y, edge_band != c)))
        def _():
            a1_copy(yy, 1).wait_send()
    m_right.wait_send()
    m_left.wait_send()
    h_right.wait_send()
    h_left.wait_send()

    @pl.when(gathers)
    def _():
        for d in range(1, nz):
            remote(tbuf.at[rr], tbuf.at[rr], a2s.at[d], a2r.at[rr], y * nz + (z + d) % nz, c).wait_send()
        for ch in range(nc):
            @pl.when(jnp.logical_or(src_row != t, ch != c))
            def _():
                c2_copy(ch).wait_send()
    for k in range(nrow):
        zk = (rb * c + 2 * nz - 1 + k) % nz

        @pl.when(zk != z)
        def _():
            remote(ubuf.at[k], cbuf.at[z], c1s.at[k], c1r.at[z], y * nz + zk, c).wait_send()


def shards_fn(nt, nz, nc, data, basis, templates, spike_offset, spike_unit, spike_amp, seg_count, neighbors):
    group, seg = data.shape
    nb, taps = basis.shape
    slots = spike_offset.shape[0]
    ny = nt // nz
    rb = nt // nc
    nrow = rb + 2
    row_units = nc * PER
    width = nb * LANES
    dma = pltpu.SemaphoreType.DMA
    vmem = pl.BlockSpec(memory_space=pltpu.VMEM)
    return pl.pallas_call(
        functools.partial(kernel, nt, nz, nc, group, taps),
        out_shape=(
            jax.ShapeDtypeStruct(data.shape, BF),
            jax.ShapeDtypeStruct(templates.shape, F32),
        ),
        in_specs=[vmem] * 7 + [pl.BlockSpec(memory_space=pl.ANY)],
        out_specs=(vmem, vmem),
        scratch_shapes=[
            pltpu.VMEM((nrow * row_units, NBR), I32),
            pltpu.VMEM((row_units, NBR), I32),
            pltpu.VMEM((8, 2 * LANES), F32),
            pltpu.VMEM((8, LANES), F32),
            pltpu.VMEM((2, 8, LANES), F32),
            pltpu.VMEM((2, 8, LANES), F32),
            pltpu.VMEM((2, group // 4, LANES), BF),
            pltpu.VMEM((2, group // 4, LANES), BF),
            pltpu.VMEM((8, LANES), F32),
            pltpu.VMEM((8 * nc, LANES), F32),
            pltpu.VMEM((nb, 2 * LANES, 2 * LANES), BF),
            pltpu.VMEM((width, 2 * LANES), BF),
            pltpu.VMEM((group, LANES), BF),
            pltpu.VMEM((group, width), BF),
            pltpu.VMEM((group, 2 * LANES), BF),
            pltpu.VMEM((nrow, 2 * nc, width // 2), BF),
            pltpu.VMEM((nrow, 2 * nc, width // 2 + LANES), BF),
            pltpu.VMEM((nz, 2 * nc, width // 2 + LANES), BF),
            pltpu.VMEM((8 * nc, LANES), F32),
            pltpu.VMEM((16 * ny, LANES), F32),
            dma((4,)),
            dma((2,)), dma((2,)), dma((2,)), dma((2,)),
            dma((2 * ny,)), dma((nc,)),
            dma((nz,)), dma((nrow,)),
            dma((nrow,)), dma((nz,)),
            dma((nc,)), dma((2 * ny,)),
        ],
        compiler_params=pltpu.CompilerParams(collective_id=0, has_side_effects=True),
        name="step",
    )(
        data, basis, templates,
        spike_offset.reshape(1, slots), spike_unit.reshape(1, slots), spike_amp.reshape(1, slots),
        seg_count.reshape(1, 1), neighbors,
    )


def solution(mesh, nz=16):
    nt, nc = mesh.shape["tm"], mesh.shape["chan"]
    return jax.shard_map(
        functools.partial(shards_fn, nt, nz, nc),
        mesh=mesh,
        in_specs=(
            P("chan", "tm"),
            P(),
            P(("tm", "chan"), None),
            P("tm"),
            P("tm"),
            P("tm"),
            P("tm"),
            P(),
        ),
        out_specs=(P("chan", "tm"), P(("tm", "chan"), None)),
        check_vma=False,
    )
```

time: 747 us -> 55.1 us (0.07)
  waiting for transfers between devices: 566 us -> 0 us
  blocking collectives: 107 us -> 0 us
  Pallas kernels: 0 us -> 49.1 us
  local copies, waits for them, and re-layouts: 37.2 us -> 4.48 us
  between operations: 15.1 us -> 1.29 us
  starting transfers between devices: 7.97 us -> 0 us
    psum x1 -> x0, waiting for transfers between devices: 374 us -> none  [shards(): total_sums, total_counts = lax.psum((unit_sums, counts), ('tm', 'chan'))]
    all_gather x1 -> x0, waiting for transfers between devices: 186 us -> none  [shards(): all_coef = lax.all_gather(templates, ('tm', 'chan'), axis=0, tiled=True)]
    psum x1 -> x0, blocking collectives: 107 us -> none  [shards(): total_sums, total_counts = lax.psum((unit_sums, counts), ('tm', 'chan'))]
    pallas_call x0 -> x1, Pallas kernels: none -> 49.1 us  [shards_fn(): pl.pallas_call(functools.partial(kernel, nt, nz, nc, group, taps), out_sh...]
    gather x9 -> x0, local copies, waits for them, and re-layouts: 28.3 us -> none  [the longest x6 27 us: shifted_basis(): picked = jnp.take(basis_low, jnp.clip(lag_index, 0, tap_count - 1), axis=1)]
    ppermute x4 -> x0, starting transfers between devices: 7.89 us -> none  [the longest x2 5.31 us: extended(): before = lax.ppermute(last, axis, up)]
  transfers between devices with their start and end apart: 6 -> 0, of which waited for: 5 -> 0; matrix products, arithmetic and copies ran while one was open for 3% -> 0% of each run, Pallas kernels for 0% -> 0%
where the time goes in v1:
time: 55.1 us; the launch traced here: 54.9 us
  Pallas kernels  49.1 us (89%)
  local copies, waits for them, and re-layouts  4.48 us (8%)
  between operations  1.29 us (2%)
    pallas_call x1, Pallas kernels, shards_fn(): pl.pallas_call(functools.partial(kernel, nt, nz, nc, group, taps), out_sh...  49.1 us
    unnamed x5, local copies, waits for them, and re-layouts  4.48 us

profile of v1, /device:TPU:1, one launch (start us, length us, event | category | flops | bytes accessed | tf_op | source)
XLA Modules:
  0.0 54.9 jit_solution(9210533861941598615)
XLA Ops:
  1.3 2.3 %copy.10.nbr = s32[2048,32]{1,0:T(8,128)} copy(s32[2048,32]{0,1:T(8,128)} %param.15) | data formatting | bytes 524288 | tf_op args[7]
  3.5 49.1 %step.1 = (bf16[768,128]{1,0:T(8,128)(2,1)}, f32[4,192]{1,0:T(4,128)}) custom-call(bf16[768,128]{1,0:T(8,128)(2,1)} %data.1, f32[6,61]{1,0:T(8,128)} %basis.1, f32[4,192]{1,0:T(4,128)} %templ.1, s32[1,32]{1,0:T(1,128)} %bitcast.5, s32[1,32]{1,0:T(1,128)} %bitcast.6, f32[1,32]{1,0:T(1,128)} %bitcast.7, s32[1,1]{1,0:T(1,128)} %bitcast.4.count, ...), custom_call_target="tpu_custom_call" | custom-call | tf_op jit(solution)/shard_map/step/pallas_call | solution.py:436
  52.7 0.0 copy-start
  52.7 1.6 %copy.14 = bf16[768,128]{1,0:T(8,128)(2,1)} copy(bf16[768,128]{1,0:T(8,128)(2,1)} %get-tuple-element.4) | data formatting | bytes 393216
  54.3 0.0 copy-done
  54.3 0.6 %copy.15 = f32[4,192]{1,0:T(4,128)} copy(f32[4,192]{1,0:T(4,128)S(1)} %copy-done) | data formatting | bytes 6144
Async XLA Ops:
  52.7 1.6 %copy-start = (f32[4,192]{1,0:T(4,128)S(1)}, f32[4,192]{1,0:T(4,128)}, u32[]{:S(2)}) copy-start(f32[4,192]{1,0:T(4,128)} %get-tuple-element.5) | copy-start | bytes 9220

commit v2 on v1

v2 whole, which is shorter than its diff:
```python
import functools

import jax
import jax.numpy as jnp
from jax import lax
from jax.experimental import pallas as pl
from jax.experimental.pallas import tpu as pltpu
from jax.sharding import PartitionSpec as P

MESH = pl.DeviceIdType.MESH
HI = lax.Precision.HIGHEST
BF = jnp.bfloat16
F32 = jnp.float32
I32 = jnp.int32
prior_weight = 4.0
LANES = 128
PER = 4
NBR = 32


def iota(shape, dim):
    return lax.broadcasted_iota(I32, shape, dim)


def dot(a, b, dims=((1,), (0,)), precision=None):
    return lax.dot_general(a, b, (dims, ((), ())), precision=precision, preferred_element_type=F32)


def one(mask, dtype=F32):
    return jnp.where(mask, 1.0, 0.0).astype(dtype)


def kernel(
    nt, nz, nc, group, taps,
    data_h, basis_h, templ_h, off_h, unit_h, amp_h, count_h, nbr_h,
    res_h, new_out,
    data, basis, templ, off, unit, amp, count, nbv, res_out, bp, mrow, msend, mrecv, hsend, hrecv, asrc, abuf, toep, shifted, maskc, placed, res,
    tbuf, ubuf, rbuf, cbuf, csrc, dbuf,
    nsem, vouch, msem_s, msem_r, hsem_s, hsem_r, a1s, a1r, a2s, a2r, c1s, c1r, c1q, c2s, c2r,
):
    ny = nt // nz
    rb = nt // nc
    nrow = rb + 2
    row_units = nc * PER
    nb = basis_h.shape[0]
    half = (taps - 1) // 2
    hop = nz // 4
    quarter = group // 4
    shards = nrow * nc
    width = nb * LANES
    t = lax.axis_index("tm")
    c = lax.axis_index("chan")
    y = t // nz
    z = t % nz
    band = t // rb
    at_low = (t % rb) == 0
    at_high = (t % rb) == rb - 1
    edge = jnp.logical_or(at_low, at_high)
    edge_band = jnp.where(at_low, (band + nc - 1) % nc, (band + 1) % nc)
    rr = (z + 2 * nz - (rb * c - 1) % nz) % nz
    gathers = rr < nrow
    src_row = (rb * c + nt - 1 + rr) % nt
    right = (t + 1) % nt
    left = (t + nt - 1) % nt

    barrier = pltpu.get_barrier_semaphore()

    def greet(tm, chan):
        pl.semaphore_signal(barrier, inc=1, device_id=(tm, chan), device_id_type=MESH)

    for d in range(1, hop + 1):
        greet(y * nz + (z + d) % nz, c)
        greet(y * nz + (z + nz - d) % nz, c)
    greet(right, c)
    greet(left, c)
    n_greet = 2 * hop + 2 + jnp.where(edge, 2 * ny, ny) + jnp.where(gathers, nc, 0)
    own_main = band == c
    own_edge = jnp.logical_and(edge, edge_band == c)
    n_greet = n_greet - jnp.where(jnp.logical_or(own_main, own_edge), 1, 0)
    n_greet = n_greet - jnp.where(jnp.logical_and(gathers, src_row == t), 1, 0)
    for yy in range(ny):
        @pl.when(jnp.logical_or(yy != y, band != c))
        def _():
            greet(yy * nz + z, band)

        @pl.when(jnp.logical_and(edge, jnp.logical_or(yy != y, edge_band != c)))
        def _():
            greet(yy * nz + z, edge_band)
    for ch in range(nc):
        @pl.when(jnp.logical_and(gathers, jnp.logical_or(src_row != t, ch != c)))
        def _():
            greet(src_row, ch)

    def fetch(src, dst, i):
        return pltpu.make_async_copy(src, dst, nsem.at[i])

    small = [
        fetch(nbr_h.at[pl.ds(0, 8), :], nbv, 0),
        fetch(templ_h, templ, 1),
        fetch(off_h, off, 2),
        fetch(unit_h, unit, 3),
        fetch(amp_h, amp, 4),
        fetch(count_h, count, 5),
    ]
    for cp in small:
        cp.start()
    bp[...] = jnp.zeros_like(bp)
    get_data = fetch(data_h, data, 6)
    get_basis = fetch(basis_h, basis, 7)
    get_data.start()
    get_basis.start()
    mrow[...] = jnp.zeros_like(mrow)

    def parts(v):
        p0 = v.astype(BF)
        p1 = (v - p0.astype(F32)).astype(BF)
        p2 = (v - p0.astype(F32) - p1.astype(F32)).astype(BF)
        return jnp.concatenate([p0.astype(F32), p1.astype(F32), p2.astype(F32)], axis=0).astype(BF)

    def joined(v):
        n = v.shape[0] // 3
        return v[:n] + v[n:2 * n] + v[2 * n:]

    for cp in small:
        cp.wait()
    lane8 = iota((8, LANES), 1)
    row8 = iota((8, LANES), 0)
    lane_u = lane8 // NBR
    first = PER * (nc * t + c)
    mine = nbv[:, pl.ds(pl.multiple_of((first // LANES) * LANES, LANES), LANES)]
    mine = pltpu.roll(mine, (LANES - first % LANES) % LANES, 1)
    s_lane = jnp.zeros((1, LANES), I32)
    for u in range(PER):
        s_lane = s_lane + jnp.where(lane_u[0:1] == u, mine[0:1, u:u + 1], 0)
    coef = nb * NBR
    turn = one(((iota((coef, LANES), 0) + s_lane - iota((coef, LANES), 1)) & (NBR - 1)) == 0, BF)
    q_of = iota((8, coef), 1) // NBR
    b_of = iota((8, coef), 0)
    spread = jnp.concatenate([jnp.where(q_of == b_of, templ[u:u + 1, :], 0.0) for u in range(PER)], axis=0)
    turned = joined(dot(parts(spread), turn))
    tblk = jnp.zeros((8, LANES), F32)
    for u in range(PER):
        tblk = tblk + jnp.where(lane_u == u, turned[8 * u:8 * u + 8, :], 0.0)
    asrc[...] = tblk

    slots = off.shape[1]
    live = (iota((1, slots), 1) < count[...]).astype(F32)
    mrow[0:1, 0:slots] = unit[...].astype(F32)
    mrow[1:2, 0:slots] = off[...].astype(F32)
    mrow[2:3, 0:slots] = jnp.where(live > 0.0, amp[...], 0.0)
    mrow[3:4, 0:slots] = live
    meta = mrow[...]
    go_right = jnp.where(t == nt - 1, 0.0, 1.0)
    go_left = jnp.where(t == 0, 0.0, 1.0)
    seg = data_h.shape[1]
    to_right = jnp.where(row8 == 1, meta - float(seg), jnp.where(row8 >= 2, meta * go_right, meta))
    to_left = jnp.where(row8 == 1, meta + float(seg), jnp.where(row8 >= 2, meta * go_left, meta))
    to_right = jnp.where(lane8 < slots, to_right, 0.0)
    to_left = jnp.where(lane8 < slots, to_left, 0.0)
    msend[0] = pltpu.roll(to_right, slots, 1)
    msend[1] = pltpu.roll(to_left, 2 * slots, 1)

    pl.semaphore_wait(barrier, n_greet)
    for d in (hop, nz - hop):
        pl.semaphore_signal(vouch, inc=1, device_id=(y * nz + (z + d) % nz, c), device_id_type=MESH)

    def remote(src, dst, s, r, tm, chan):
        return pltpu.make_async_remote_copy(
            src_ref=src, dst_ref=dst, send_sem=s, recv_sem=r, device_id=(tm, chan), device_id_type=MESH
        )

    def block8(ref, i):
        return ref.at[pl.ds(pl.multiple_of(8 * i, 8), 8), :]

    def a1_copy(yy, e):
        return remote(asrc, block8(abuf, c), a1s.at[e * ny + yy], a1r.at[c], yy * nz + z, edge_band if e else band)

    for yy in range(ny):
        @pl.when(jnp.logical_or(yy != y, band != c))
        def _():
            a1_copy(yy, 0).start()

        @pl.when(jnp.logical_and(edge, jnp.logical_or(yy != y, edge_band != c)))
        def _():
            a1_copy(yy, 1).start()

    @pl.when(jnp.logical_or(own_main, own_edge))
    def _():
        block8(abuf, c)[...] = asrc[...]

    m_right = remote(msend.at[0], mrecv.at[0], msem_s.at[0], msem_r.at[0], right, c)
    m_left = remote(msend.at[1], mrecv.at[1], msem_s.at[1], msem_r.at[1], left, c)
    h_right = remote(hsend.at[0], hrecv.at[0], hsem_s.at[0], hsem_r.at[0], right, c)
    h_left = remote(hsend.at[1], hrecv.at[1], hsem_s.at[1], hsem_r.at[1], left, c)
    m_right.start()
    m_left.start()

    get_data.wait()
    sel_i = iota((seg, 2 * LANES), 0)
    sel_j = iota((seg, 2 * LANES), 1)
    pack = jnp.zeros((quarter, 2 * LANES), F32)
    for k in range(4):
        to_r = (sel_j == sel_i - (seg - 32) + 32 * k) & (sel_i >= seg - 32)
        to_l = (sel_j == sel_i + 32 * k + LANES) & (sel_i < 32)
        pack = pack + dot(data[k * quarter:(k + 1) * quarter, :], one(to_r | to_l, BF))
    hsend[0] = pack[:, :LANES].astype(BF)
    hsend[1] = pack[:, LANES:].astype(BF)

    h_right.start()
    h_left.start()

    get_basis.wait()
    bp[0:nb, 0:taps] = basis[...]
    span = 2 * LANES
    base = 66
    lane_s = iota((LANES, LANES), 1)

    def shifts(b):
        row = jnp.broadcast_to(bp[b:b + 1, :].astype(BF).astype(F32), (LANES, span))
        for r0 in (0, LANES):
            mid = pltpu.roll(row, (span - half - base + r0) % span, 1, stride=1, stride_axis=0)[:, :LANES]
            low = pltpu.roll(row, (span - half - base + 32 + r0) % span, 1, stride=1, stride_axis=0)[:, :LANES]
            high = pltpu.roll(row, (span - half - base - seg + 32 + r0) % span, 1, stride=1, stride_axis=0)[:, :LANES]
            side = jnp.where(lane_s < 32, low, jnp.where(lane_s < 64, high, 0.0))
            toep[b, r0:r0 + LANES, 0:LANES] = mid.astype(BF)
            toep[b, r0:r0 + LANES, LANES:span] = side.astype(BF)

    for b in range(nb):
        shifts(b)
    gram = dot(bp[...], bp[...], ((1,), (1,)), precision=HI)
    gram_t = dot(gram, tblk, precision=HI)

    pl.semaphore_wait(vouch, 2)

    @pl.when(gathers)
    def _():
        for ch in range(nc):
            @pl.when(jnp.logical_or(src_row != t, ch != c))
            def _():
                remote(asrc, block8(abuf, ch), a1s.at[0], a1r.at[ch], src_row, ch).wait_recv()
        rows = [abuf[pl.ds(b, nc, stride=8), :] for b in range(nb)]
        tbuf[rr] = jnp.concatenate(rows, axis=1).astype(BF)
        for d in [nz // 2] + [s * k for k in range(nz // 2 - 1, 0, -1) for s in (1, -1)]:
            remote(tbuf.at[rr], tbuf.at[rr], a2s.at[d % nz], a2r.at[rr], y * nz + (z + d + nz) % nz, c).start()

    m_right.wait_recv()
    m_left.wait_recv()
    every = meta + mrecv[0] + mrecv[1]
    unit_lane = every[0:1, :].astype(I32)
    shard_lane = unit_lane // PER - nc * (rb * c - 1)
    live_lane = every[3:4, :]
    stack = jnp.where(row8 == 1, every + float(base), jnp.where(row8 < 4, every, 0.0))
    cols = jnp.transpose(stack)
    unit_col = cols[:, 0:1].astype(I32)
    pos_col = cols[:, 1:2].astype(I32)
    amp_col = cols[:, 2:3]
    shard_col = unit_col // PER - nc * (rb * c - 1)
    sub_col = unit_col % PER
    n_tiles = nbv.shape[1] // LANES
    band_tiles = max(rb * row_units // LANES, 1)
    sum_start = jnp.zeros((LANES, LANES), I32)
    for k in range(min(band_tiles + 2, n_tiles)):
        tile = (c * rb * row_units // LANES - 1 + k + n_tiles) % n_tiles
        starts = nbv[:, pl.ds(pl.multiple_of(tile * LANES, LANES), LANES)][0:1]
        sum_start = sum_start + jnp.where(unit_col - tile * LANES == iota((LANES, LANES), 1), starts, 0)
    start_all = jnp.sum(sum_start.astype(F32), axis=1, keepdims=True) - float(group) * c.astype(F32)
    start_lane = jnp.transpose(jnp.broadcast_to(start_all, (LANES, LANES)))[0:1, :].astype(I32)
    start_col = start_all[0:slots].astype(I32)

    at_pos = one(pos_col == iota((LANES, span), 1), BF)
    for b in range(nb):
        shifted[b * LANES:(b + 1) * LANES, :] = dot(at_pos, toep[b]).astype(BF)
    maskc[...] = one(
        (iota((group, LANES), 0) >= start_lane) & (iota((group, LANES), 0) < start_lane + NBR), BF
    )
    own_mask = one((iota((slots, group), 1) >= start_col) & (iota((slots, group), 1) < start_col + NBR))
    shard_n = one(shard_col == iota((LANES, shards), 1), BF)
    n_shard = one(shard_lane == iota((shards, LANES), 0)) * live_lane
    lane_sub = iota((LANES, LANES), 1) // NBR
    weigh = jnp.where(lane_sub == sub_col, amp_col, 0.0)
    fold = one((iota((NBR, LANES), 1) & (NBR - 1)) == iota((NBR, LANES), 0), BF)
    spin = one((iota((LANES, LANES), 1) & (NBR - 1)) == (iota((LANES, LANES), 0) & (NBR - 1)), BF)
    sub_own = one(lane_sub == sub_col)[0:slots, :]

    l_i = iota((LANES, LANES), 1)
    tally_w = jnp.where(l_i < PER, one(l_i == sub_col), 0.0)
    tally_w = tally_w + jnp.where((l_i >= PER) & (l_i < 3 * PER), one((l_i & (PER - 1)) == sub_col) * amp_col, 0.0)
    tally_w = jnp.where(iota((LANES, LANES), 0) < slots, tally_w, 0.0)
    tally = dot(n_shard, tally_w, precision=HI)
    t_i = iota((shards, LANES), 0)
    tally = jnp.where((t_i >= nc) & (t_i < nc * (rb + 1)), tally, 0.0)
    coarse = tally.astype(BF).astype(F32)
    tally = jnp.where(iota((shards, LANES), 1) < 2 * PER, coarse, tally - coarse)

    h_right.wait_recv()
    h_left.wait_recv()
    un_i = iota((LANES, LANES), 0)
    un_j = iota((LANES, LANES), 1)
    wings = []
    for k in range(4):
        from_l = one((un_i == un_j + 32 * k) & (un_j < 32), BF)
        from_r = one((un_i == un_j - 32 + 32 * k) & (un_j >= 32) & (un_j < 64), BF)
        wings.append(dot(hrecv[0], from_l) + dot(hrecv[1], from_r))
    wing = jnp.concatenate(wings, axis=0)
    wing_lane = iota((group, LANES), 1)
    inside = ((wing_lane < 32) & (t > 0)) | ((wing_lane >= 32) & (wing_lane < 64) & (t < nt - 1))

    for k in range(nrow):
        zk = (rb * c + 2 * nz - 1 + k) % nz

        @pl.when(zk != z)
        def _():
            remote(tbuf.at[k], tbuf.at[k], a2s.at[0], a2r.at[k], y * nz + zk, c).wait_recv()
    blocks = [tbuf[k].astype(F32) for k in range(nrow)]
    chosen = dot(shard_n, jnp.concatenate(blocks, axis=0).astype(BF))
    for b in range(nb):
        low = (chosen[:, b * LANES:(b + 1) * LANES] * weigh).astype(BF)
        lowt = dot(fold, low, ((1,), (1,))).astype(BF)
        placed[:, b * LANES:(b + 1) * LANES] = jnp.concatenate([lowt] * (group // NBR), axis=0) * maskc[...]
    model = dot(placed[...], shifted[...])
    centre = (data[...].astype(F32) - model[:, :LANES]).astype(BF)
    res_out[...] = centre
    put_res = fetch(res_out, res_h, 8)
    put_res.start()
    res[:, 0:LANES] = centre
    res[:, LANES:span] = jnp.where(inside, wing - model[:, LANES:], 0.0).astype(BF)

    own_shift = jnp.concatenate([shifted[b * LANES:b * LANES + slots, :] for b in range(nb)], axis=0)
    along = dot(own_shift, res[...], ((1,), (1,)))
    own_all = jnp.concatenate([own_mask] * nb, axis=0)
    hit = along * own_all
    feat = hit[:, 0:LANES]
    for k in range(1, group // LANES):
        feat = feat + hit[:, k * LANES:(k + 1) * LANES]
    feat = dot(feat.astype(BF), spin)
    spread_w = jnp.concatenate([feat[b * slots:(b + 1) * slots, :] * sub_own for b in range(nb)], axis=1)
    sums = dot(n_shard[:, 0:slots].astype(BF), spread_w.astype(BF))
    for k in range(nrow):
        lo, hi = k * nc, (k + 1) * nc
        ubuf[k] = jnp.concatenate([sums[lo:hi, :], tally[lo:hi, :]], axis=1).astype(BF)

    def z_of(k):
        return (rb * c + 2 * nz - 1 + k) % nz

    def to_relay(f):
        for k in range(nrow):
            dist = (z - z_of(k) + nz) % nz

            @pl.when(jnp.logical_and(dist > hop, dist <= 2 * hop))
            def _():
                at = y * nz + (z_of(k) + hop) % nz
                f(remote(ubuf.at[k], rbuf.at[dist - hop - 1], c1s.at[k], c1q.at[dist - hop - 1], at, c))

            @pl.when(jnp.logical_and(dist > 2 * hop, dist < 3 * hop))
            def _():
                at = y * nz + (z_of(k) + nz - hop) % nz
                i = 4 * hop - 1 - dist
                f(remote(ubuf.at[k], rbuf.at[i], c1s.at[k], c1q.at[i], at, c))

    def near_slot(dist):
        return jnp.where(dist <= hop, dist - 1, dist - 2 * hop)

    def to_gatherer(f):
        for k in range(nrow):
            dist = (z - z_of(k) + nz) % nz

            @pl.when(jnp.logical_or(jnp.logical_and(dist >= 1, dist < hop), dist > 3 * hop))
            def _():
                i = near_slot(dist)
                f(remote(ubuf.at[k], cbuf.at[i], c1s.at[k], c1r.at[i], y * nz + z_of(k), c))

    relays = ((hop, 0, hop), (3 * hop, hop, 2 * hop - 1))

    def relay_copy(dist):
        zt = (z - dist + nz) % nz
        k = (zt + 2 * nz - (rb * c - 1) % nz) % nz
        i = hop - 1 if dist == hop else hop
        return k, remote(ubuf.at[k], cbuf.at[i], c1s.at[k], c1r.at[i], y * nz + zt, c)

    to_relay(lambda cp: cp.start())
    to_gatherer(lambda cp: cp.start())
    for dist, lo, hi in relays:
        k, out = relay_copy(dist)

        @pl.when(k < nrow)
        def _():
            for j in range(lo, hi):
                remote(ubuf.at[0], rbuf.at[j], c1s.at[0], c1q.at[j], y * nz + (z + 1) % nz, c).wait_recv()
            part = ubuf[k].astype(F32)
            for j in range(lo, hi):
                part = part + rbuf[j].astype(F32)
            ubuf[k] = part.astype(BF)
            out.start()

    to_edge = jnp.logical_or(rr == 0, rr == nrow - 1)
    slot_out = jnp.where(to_edge, ny, 0) + y

    def c2_copy(ch):
        return remote(block8(csrc, ch), block8(dbuf, slot_out), c2s.at[ch], c2r.at[slot_out], src_row, ch)

    @pl.when(jnp.logical_not(edge))
    def _():
        dbuf[8 * ny:16 * ny, :] = jnp.zeros((8 * ny, LANES), F32)

    @pl.when(gathers)
    def _():
        for i in [j for j in range(2 * hop) if j not in (hop - 1, hop)] + [hop - 1, hop]:
            remote(ubuf.at[0], cbuf.at[i], c1s.at[0], c1r.at[i], y * nz + (z + 1) % nz, c).wait_recv()
        total = ubuf[rr].astype(F32)
        for k in range(2 * hop):
            total = total + cbuf[k].astype(F32)
        for b in range(nb + 1):
            csrc[pl.ds(b, nc, stride=8), :] = total[:, b * LANES:(b + 1) * LANES]
        csrc[pl.ds(nb + 1, nc, stride=8), :] = jnp.zeros((nc, LANES), F32)
        for ch in range(nc):
            is_own = jnp.logical_and(src_row == t, ch == c)

            @pl.when(jnp.logical_not(is_own))
            def _():
                c2_copy(ch).start()

            @pl.when(is_own)
            def _():
                block8(dbuf, slot_out)[...] = csrc[8 * ch:8 * ch + 8, :]

    for yy in range(ny):
        @pl.when(jnp.logical_or(yy != y, band != c))
        def _():
            remote(block8(csrc, 0), block8(dbuf, yy), c2s.at[0], c2r.at[yy], yy * nz + z, band).wait_recv()

        @pl.when(jnp.logical_and(edge, jnp.logical_or(yy != y, edge_band != c)))
        def _():
            remote(
                block8(csrc, 0), block8(dbuf, ny + yy), c2s.at[0], c2r.at[ny + yy], yy * nz + z, edge_band
            ).wait_recv()
    got = dbuf[0:8, :]
    for k in range(1, 2 * ny):
        got = got + dbuf[8 * k:8 * k + 8, :]
    tail = got[nb:nb + 1, :]
    number = jnp.zeros((1, LANES), F32)
    weight = jnp.zeros((1, LANES), F32)
    for u in range(PER):
        here = lane_u[0:1] == u
        number = number + jnp.where(here, tail[:, u:u + 1], 0.0)
        weight = weight + jnp.where(here, tail[:, PER + u:PER + u + 1] + tail[:, 2 * PER + u:2 * PER + u + 1], 0.0)
    fresh = (prior_weight * tblk + got + weight * gram_t) / (prior_weight + number)
    split = jnp.concatenate([jnp.where(lane_u == u, fresh, 0.0) for u in range(PER)], axis=0)
    back = joined(dot(parts(split), turn, ((1,), (1,))))
    for u in range(PER):
        piece = jnp.where(q_of == b_of, back[8 * u:8 * u + 8, :], 0.0)
        new_out[u:u + 1, :] = jnp.sum(piece, axis=0, keepdims=True)

    for yy in range(ny):
        @pl.when(jnp.logical_or(yy != y, band != c))
        def _():
            a1_copy(yy, 0).wait_send()

        @pl.when(jnp.logical_and(edge, jnp.logical_or(yy != y, edge_band != c)))
        def _():
            a1_copy(yy, 1).wait_send()
    m_right.wait_send()
    m_left.wait_send()
    h_right.wait_send()
    h_left.wait_send()

    @pl.when(gathers)
    def _():
        for d in range(1, nz):
            remote(tbuf.at[rr], tbuf.at[rr], a2s.at[d], a2r.at[rr], y * nz + (z + d) % nz, c).wait_send()
        for ch in range(nc):
            @pl.when(jnp.logical_or(src_row != t, ch != c))
            def _():
                c2_copy(ch).wait_send()
    to_relay(lambda cp: cp.wait_send())
    to_gatherer(lambda cp: cp.wait_send())
    for dist, lo, hi in relays:
        k, out = relay_copy(dist)

        @pl.when(k < nrow)
        def _():
            out.wait_send()
    put_res.wait()


def shards_fn(nt, nz, nc, data, basis, templates, spike_offset, spike_unit, spike_amp, seg_count, neighbors):
    group, seg = data.shape
    nb, taps = basis.shape
    slots = spike_offset.shape[0]
    ny = nt // nz
    rb = nt // nc
    nrow = rb + 2
    row_units = nc * PER
    width = nb * LANES
    dma = pltpu.SemaphoreType.DMA
    vmem = pl.BlockSpec(memory_space=pltpu.VMEM)
    hbm = pl.BlockSpec(memory_space=pl.ANY)
    hop = nz // 4
    return pl.pallas_call(
        functools.partial(kernel, nt, nz, nc, group, taps),
        out_shape=(
            jax.ShapeDtypeStruct(data.shape, BF),
            jax.ShapeDtypeStruct(templates.shape, F32),
        ),
        in_specs=[hbm] * 8,
        out_specs=(hbm, vmem),
        scratch_shapes=[
            pltpu.VMEM(data.shape, BF),
            pltpu.VMEM(basis.shape, F32),
            pltpu.VMEM(templates.shape, F32),
            pltpu.VMEM((1, slots), I32),
            pltpu.VMEM((1, slots), I32),
            pltpu.VMEM((1, slots), F32),
            pltpu.VMEM((1, 1), I32),
            pltpu.VMEM((8, neighbors.shape[0]), I32),
            pltpu.VMEM(data.shape, BF),
            pltpu.VMEM((8, 2 * LANES), F32),
            pltpu.VMEM((8, LANES), F32),
            pltpu.VMEM((2, 8, LANES), F32),
            pltpu.VMEM((2, 8, LANES), F32),
            pltpu.VMEM((2, group // 4, LANES), BF),
            pltpu.VMEM((2, group // 4, LANES), BF),
            pltpu.VMEM((8, LANES), F32),
            pltpu.VMEM((8 * nc, LANES), F32),
            pltpu.VMEM((nb, 2 * LANES, 2 * LANES), BF),
            pltpu.VMEM((width, 2 * LANES), BF),
            pltpu.VMEM((group, LANES), BF),
            pltpu.VMEM((group, width), BF),
            pltpu.VMEM((group, 2 * LANES), BF),
            pltpu.VMEM((nrow, nc, width), BF),
            pltpu.VMEM((nrow, nc, width + LANES), BF),
            pltpu.VMEM((2 * hop - 1, nc, width + LANES), BF),
            pltpu.VMEM((2 * hop, nc, width + LANES), BF),
            pltpu.VMEM((8 * nc, LANES), F32),
            pltpu.VMEM((16 * ny, LANES), F32),
            dma((9,)), pltpu.SemaphoreType.REGULAR,
            dma((2,)), dma((2,)), dma((2,)), dma((2,)),
            dma((2 * ny,)), dma((nc,)),
            dma((nz,)), dma((nrow,)),
            dma((nrow,)), dma((2 * hop,)), dma((2 * hop - 1,)),
            dma((nc,)), dma((2 * ny,)),
        ],
        compiler_params=pltpu.CompilerParams(collective_id=0, has_side_effects=True),
        name="step",
    )(
        data, basis, templates,
        spike_offset.reshape(1, slots), spike_unit.reshape(1, slots), spike_amp.reshape(1, slots),
        seg_count.reshape(1, 1), neighbors.T,
    )


def solution(mesh, nz=16):
    nt, nc = mesh.shape["tm"], mesh.shape["chan"]
    return jax.shard_map(
        functools.partial(shards_fn, nt, nz, nc),
        mesh=mesh,
        in_specs=(
            P("chan", "tm"),
            P(),
            P(("tm", "chan"), None),
            P("tm"),
            P("tm"),
            P("tm"),
            P("tm"),
            P(),
        ),
        out_specs=(P("chan", "tm"), P(("tm", "chan"), None)),
        check_vma=False,
    )
```

time: 55.1 us -> 50.4 us (0.915)
  Pallas kernels: 49.1 us -> 46.7 us
  local copies, waits for them, and re-layouts: 4.48 us -> 2.21 us
    pallas_call x1, Pallas kernels: 49.1 us -> 46.7 us  [shards_fn(): pl.pallas_call(functools.partial(kernel, nt, nz, nc, group, taps), out_sh...]
    unnamed x5 -> x4, local copies, waits for them, and re-layouts: 4.48 us -> 2.21 us
where the time goes in v2:
time: 50.4 us; the launch traced here: 50.3 us
  Pallas kernels  46.7 us (93%)
  local copies, waits for them, and re-layouts  2.21 us (4%)
  between operations  1.3 us (3%)
    pallas_call x1, Pallas kernels, shards_fn(): pl.pallas_call(functools.partial(kernel, nt, nz, nc, group, taps), out_sh...  46.7 us
    unnamed x4, local copies, waits for them, and re-layouts  2.21 us

profile of v2, /device:TPU:1, one launch (start us, length us, event | category | flops | bytes accessed | tf_op | source)
XLA Modules:
  0.0 50.3 jit_solution(6247087271956080240)
XLA Ops:
  1.3 46.7 %step.1 = (bf16[768,128]{1,0:T(8,128)(2,1)}, f32[4,192]{1,0:T(4,128)}) custom-call(bf16[768,128]{1,0:T(8,128)(2,1)} %data_h.1, f32[6,61]{1,0:T(8,128)} %basis_h.1, f32[4,192]{1,0:T(4,128)} %templ_h.1, s32[1,32]{1,0:T(1,128)} %bitcast.7, s32[1,32]{1,0:T(1,128)} %bitcast.8, f32[1,32]{1,0:T(1,128)} %bitcast.9, s32[1,1]{1,0:T(1,128)} %bitcast.5.count_h, ...), custom_call_target="tpu_custom_call" | custom-call | tf_op jit(solution)/shard_map/step/pallas_call | solution.py:498
  48.0 0.0 copy-start
  48.0 1.6 %copy.13 = bf16[768,128]{1,0:T(8,128)(2,1)} copy(bf16[768,128]{1,0:T(8,128)(2,1)} %get-tuple-element.4) | data formatting | bytes 393216
  49.7 0.0 copy-done
  49.7 0.6 %copy.14 = f32[4,192]{1,0:T(4,128)} copy(f32[4,192]{1,0:T(4,128)S(1)} %copy-done) | data formatting | bytes 6144
Async XLA Ops:
  48.0 1.6 %copy-start = (f32[4,192]{1,0:T(4,128)S(1)}, f32[4,192]{1,0:T(4,128)}, u32[]{:S(2)}) copy-start(f32[4,192]{1,0:T(4,128)} %get-tuple-element.5) | copy-start | bytes 9220

commit v3 on v2

--- a/solution.py
+++ b/solution.py
@@ -319,9 +319,7 @@
         placed[:, b * LANES:(b + 1) * LANES] = jnp.concatenate([lowt] * (group // NBR), axis=0) * maskc[...]
     model = dot(placed[...], shifted[...])
     centre = (data[...].astype(F32) - model[:, :LANES]).astype(BF)
-    res_out[...] = centre
-    put_res = fetch(res_out, res_h, 8)
-    put_res.start()
+    res_h[...] = centre
     res[:, 0:LANES] = centre
     res[:, LANES:span] = jnp.where(inside, wing - model[:, LANES:], 0.0).astype(BF)
 
@@ -479,7 +477,6 @@
         @pl.when(k < nrow)
         def _():
             out.wait_send()
-    put_res.wait()
 
 
 def shards_fn(nt, nz, nc, data, basis, templates, spike_offset, spike_unit, spike_amp, seg_count, neighbors):
@@ -498,11 +495,11 @@
     return pl.pallas_call(
         functools.partial(kernel, nt, nz, nc, group, taps),
         out_shape=(
-            jax.ShapeDtypeStruct(data.shape, BF),
-            jax.ShapeDtypeStruct(templates.shape, F32),
+            pltpu.VMEM(data.shape, BF),
+            pltpu.VMEM(templates.shape, F32),
         ),
         in_specs=[hbm] * 8,
-        out_specs=(hbm, vmem),
+        out_specs=(vmem, vmem),
         scratch_shapes=[
             pltpu.VMEM(data.shape, BF),
             pltpu.VMEM(basis.shape, F32),

time: 50.4 us -> 48.8 us (0.968)
  local copies, waits for them, and re-layouts: 2.21 us -> 1.27 us
  Pallas kernels: 46.7 us -> 46.1 us
    unnamed x4 -> x2, local copies, waits for them, and re-layouts: 2.21 us -> 1.27 us
    pallas_call x1, Pallas kernels: 46.7 us -> 46.1 us  [shards_fn(): pl.pallas_call(functools.partial(kernel, nt, nz, nc, group, taps), out_sh...]
where the time goes in v3:
time: 48.8 us; the launch traced here: 48.7 us
  Pallas kernels  46.1 us (94%)
  between operations  1.29 us (3%)
  local copies, waits for them, and re-layouts  1.27 us (3%)
    pallas_call x1, Pallas kernels, shards_fn(): pl.pallas_call(functools.partial(kernel, nt, nz, nc, group, taps), out_sh...  46.1 us
    unnamed x2, local copies, waits for them, and re-layouts  1.27 us

profile of v3, /device:TPU:1, one launch (start us, length us, event | category | flops | bytes accessed | tf_op | source)
XLA Modules:
  0.0 48.7 jit_solution(11816813418217489982)
XLA Ops:
  1.3 46.1 %step.1 = (bf16[768,128]{1,0:T(8,128)(2,1)S(1)}, f32[4,192]{1,0:T(4,128)S(1)}) custom-call(bf16[768,128]{1,0:T(8,128)(2,1)} %data_h.1, f32[6,61]{1,0:T(8,128)} %basis_h.1, f32[4,192]{1,0:T(4,128)} %templ_h.1, s32[1,32]{1,0:T(1,128)} %bitcast.7, s32[1,32]{1,0:T(1,128)} %bitcast.8, f32[1,32]{1,0:T(1,128)} %bitcast.9, s32[1,1]{1,0:T(1,128)} %bitcast.5.count_h, ...), custom_call_target="tpu_custom_call" | custom-call | tf_op jit(solution)/shard_map/step/pallas_call | solution.py:495
  47.4 0.7 %copy.12 = bf16[768,128]{1,0:T(8,128)(2,1)} copy(bf16[768,128]{1,0:T(8,128)(2,1)S(1)} %get-tuple-element.2) | data formatting | bytes 393216
  48.1 0.6 %copy.13 = f32[4,192]{1,0:T(4,128)} copy(f32[4,192]{1,0:T(4,128)S(1)} %get-tuple-element.3) | data formatting | bytes 6144

commit v4 on v3

--- a/solution.py
+++ b/solution.py
@@ -34,9 +34,9 @@
     nt, nz, nc, group, taps,
     data_h, basis_h, templ_h, off_h, unit_h, amp_h, count_h, nbr_h,
     res_h, new_out,
-    data, basis, templ, off, unit, amp, count, nbv, res_out, bp, mrow, msend, mrecv, hsend, hrecv, asrc, abuf, toep, shifted, maskc, placed, res,
-    tbuf, ubuf, rbuf, cbuf, csrc, dbuf,
-    nsem, vouch, msem_s, msem_r, hsem_s, hsem_r, a1s, a1r, a2s, a2r, c1s, c1r, c1q, c2s, c2r,
+    data, basis, templ, off, unit, amp, count, nbv, bp, mrow, msend, mrecv, hsend, hrecv, asrc, abuf, toep, shifted, maskc, placed, res,
+    tbuf, uf, ef, xsrc, esrc, mbuf, ebuf, zf, zsrc, zbuf,
+    nsem, vouch, msem_s, msem_r, hsem_s, hsem_r, a1s, a1r, a2s, a2r, xms, xmr, xes, xer, zss, zrs,
 ):
     ny = nt // nz
     rb = nt // nc
@@ -73,23 +73,26 @@
         greet(y * nz + (z + nz - d) % nz, c)
     greet(right, c)
     greet(left, c)
-    n_greet = 2 * hop + 2 + jnp.where(edge, 2 * ny, ny) + jnp.where(gathers, nc, 0)
+    home = c // 2
+    odd = c % 2
+    beyond = jnp.where(odd == 0, (home + ny - 1) % ny, (home + 1) % ny)
+    feeders = (2 * y, 2 * y + 1, (2 * y + 2) % nc, (2 * y + nc - 1) % nc)
+    for ch in range(nc):
+        for yo in (home, beyond):
+            @pl.when(jnp.logical_or(yo != y, ch != c))
+            def _():
+                greet(yo * nz + z, ch)
+    for yy in range(ny):
+        for src in feeders:
+            @pl.when(jnp.logical_or(yy != y, src != c))
+            def _():
+                greet(yy * nz + z, src)
+    own_home = y == home
+    own_beyond = y == beyond
+    n_greet = 2 * hop + 2 + 2 * nc + 4 * ny
+    n_greet = n_greet - jnp.where(own_home, 2, 0) - jnp.where(own_beyond, 2, 0)
     own_main = band == c
     own_edge = jnp.logical_and(edge, edge_band == c)
-    n_greet = n_greet - jnp.where(jnp.logical_or(own_main, own_edge), 1, 0)
-    n_greet = n_greet - jnp.where(jnp.logical_and(gathers, src_row == t), 1, 0)
-    for yy in range(ny):
-        @pl.when(jnp.logical_or(yy != y, band != c))
-        def _():
-            greet(yy * nz + z, band)
-
-        @pl.when(jnp.logical_and(edge, jnp.logical_or(yy != y, edge_band != c)))
-        def _():
-            greet(yy * nz + z, edge_band)
-    for ch in range(nc):
-        @pl.when(jnp.logical_and(gathers, jnp.logical_or(src_row != t, ch != c)))
-        def _():
-            greet(src_row, ch)
 
     def fetch(src, dst, i):
         return pltpu.make_async_copy(src, dst, nsem.at[i])
@@ -283,14 +286,18 @@
     sub_own = one(lane_sub == sub_col)[0:slots, :]
 
     l_i = iota((LANES, LANES), 1)
-    tally_w = jnp.where(l_i < PER, one(l_i == sub_col), 0.0)
-    tally_w = tally_w + jnp.where((l_i >= PER) & (l_i < 3 * PER), one((l_i & (PER - 1)) == sub_col) * amp_col, 0.0)
-    tally_w = jnp.where(iota((LANES, LANES), 0) < slots, tally_w, 0.0)
-    tally = dot(n_shard, tally_w, precision=HI)
-    t_i = iota((shards, LANES), 0)
-    tally = jnp.where((t_i >= nc) & (t_i < nc * (rb + 1)), tally, 0.0)
-    coarse = tally.astype(BF).astype(F32)
-    tally = jnp.where(iota((shards, LANES), 1) < 2 * PER, coarse, tally - coarse)
+    kind = (l_i & 15) // PER
+    match = ((l_i & (PER - 1)) == sub_col) & ((shard_col // nc) - 1 == l_i // 16) & (shard_col >= nc)
+    match = match & (iota((LANES, LANES), 0) < slots)
+    tally_w = jnp.where(match, jnp.where(kind == 0, 1.0, jnp.where(kind < 3, amp_col, 0.0)), 0.0)
+    n_owner = one((shard_lane & (nc - 1)) == iota((8, LANES), 0)) * live_lane
+    kind8 = (lane8 & 15) // PER
+
+    def halves(v):
+        coarse = v.astype(BF).astype(F32)
+        return jnp.where(kind8 == 2, v - coarse, coarse)
+
+    tally = halves(dot(n_owner, tally_w, precision=HI))
 
     h_right.wait_recv()
     h_left.wait_recv()
@@ -333,108 +340,101 @@
     feat = dot(feat.astype(BF), spin)
     spread_w = jnp.concatenate([feat[b * slots:(b + 1) * slots, :] * sub_own for b in range(nb)], axis=1)
     sums = dot(n_shard[:, 0:slots].astype(BF), spread_w.astype(BF))
-    for k in range(nrow):
-        lo, hi = k * nc, (k + 1) * nc
-        ubuf[k] = jnp.concatenate([sums[lo:hi, :], tally[lo:hi, :]], axis=1).astype(BF)
-
-    def z_of(k):
-        return (rb * c + 2 * nz - 1 + k) % nz
-
-    def to_relay(f):
-        for k in range(nrow):
-            dist = (z - z_of(k) + nz) % nz
-
-            @pl.when(jnp.logical_and(dist > hop, dist <= 2 * hop))
-            def _():
-                at = y * nz + (z_of(k) + hop) % nz
-                f(remote(ubuf.at[k], rbuf.at[dist - hop - 1], c1s.at[k], c1q.at[dist - hop - 1], at, c))
-
-            @pl.when(jnp.logical_and(dist > 2 * hop, dist < 3 * hop))
-            def _():
-                at = y * nz + (z_of(k) + nz - hop) % nz
-                i = 4 * hop - 1 - dist
-                f(remote(ubuf.at[k], rbuf.at[i], c1s.at[k], c1q.at[i], at, c))
-
-    def near_slot(dist):
-        return jnp.where(dist <= hop, dist - 1, dist - 2 * hop)
-
-    def to_gatherer(f):
-        for k in range(nrow):
-            dist = (z - z_of(k) + nz) % nz
-
-            @pl.when(jnp.logical_or(jnp.logical_and(dist >= 1, dist < hop), dist > 3 * hop))
-            def _():
-                i = near_slot(dist)
-                f(remote(ubuf.at[k], cbuf.at[i], c1s.at[k], c1r.at[i], y * nz + z_of(k), c))
-
-    relays = ((hop, 0, hop), (3 * hop, hop, 2 * hop - 1))
-
-    def relay_copy(dist):
-        zt = (z - dist + nz) % nz
-        k = (zt + 2 * nz - (rb * c - 1) % nz) % nz
-        i = hop - 1 if dist == hop else hop
-        return k, remote(ubuf.at[k], cbuf.at[i], c1s.at[k], c1r.at[i], y * nz + zt, c)
-
-    to_relay(lambda cp: cp.start())
-    to_gatherer(lambda cp: cp.start())
-    for dist, lo, hi in relays:
-        k, out = relay_copy(dist)
-
-        @pl.when(k < nrow)
-        def _():
-            for j in range(lo, hi):
-                remote(ubuf.at[0], rbuf.at[j], c1s.at[0], c1q.at[j], y * nz + (z + 1) % nz, c).wait_recv()
-            part = ubuf[k].astype(F32)
-            for j in range(lo, hi):
-                part = part + rbuf[j].astype(F32)
-            ubuf[k] = part.astype(BF)
-            out.start()
-
-    to_edge = jnp.logical_or(rr == 0, rr == nrow - 1)
-    slot_out = jnp.where(to_edge, ny, 0) + y
-
-    def c2_copy(ch):
-        return remote(block8(csrc, ch), block8(dbuf, slot_out), c2s.at[ch], c2r.at[slot_out], src_row, ch)
-
-    @pl.when(jnp.logical_not(edge))
+    for b in range(nb):
+        uf[b] = sums[:, b * LANES:(b + 1) * LANES]
+    first_row, last_row = sums[:nc, :], sums[(nrow - 1) * nc:, :]
+    inner = jnp.where(odd == 0, last_row, first_row)
+    outer = jnp.where(odd == 0, first_row, last_row)
+    blank = jnp.zeros((nc, LANES), F32)
+    for b in range(nb):
+        ef[0, pl.ds(b, nc, stride=8), :] = inner[:, b * LANES:(b + 1) * LANES]
+        ef[1, pl.ds(b, nc, stride=8), :] = outer[:, b * LANES:(b + 1) * LANES]
+    ef[0, pl.ds(nb, nc, stride=8), :] = tally[:nc]
+    ef[1, pl.ds(nb, nc, stride=8), :] = blank
+    for e in range(2):
+        ef[e, pl.ds(nb + 1, nc, stride=8), :] = blank
+
+    def to_home(ch):
+        return remote(xsrc.at[ch], mbuf.at[odd, y], xms.at[ch], xmr.at[odd, y], home * nz + z, ch)
+
+    def to_beyond(ch):
+        return remote(esrc.at[ch], ebuf.at[odd, y], xes.at[ch], xer.at[odd, y], beyond * nz + z, ch)
+
+    def to_owners(f):
+        for ch in range(nc):
+            @pl.when(jnp.logical_or(y != home, ch != c))
+            def _():
+                f(to_home(ch))
+        for ch in range(nc):
+            @pl.when(jnp.logical_or(y != beyond, ch != c))
+            def _():
+                f(to_beyond(ch))
+
+    for ch in range(nc):
+        pieces = [uf[b, pl.ds(nc + ch, rb, stride=nc), :] for b in range(nb)] + [ef[0, 8 * ch:8 * ch + 8, :]]
+        xsrc[ch] = jnp.concatenate(pieces, axis=0).astype(BF)
+        esrc[ch] = ef[1, 8 * ch:8 * ch + 8, :].astype(BF)
+    to_owners(lambda cp: cp.start())
+
+    @pl.when(own_home)
     def _():
-        dbuf[8 * ny:16 * ny, :] = jnp.zeros((8 * ny, LANES), F32)
-
-    @pl.when(gathers)
+        mbuf[odd, y] = xsrc[c]
+
+    @pl.when(own_beyond)
     def _():
-        for i in [j for j in range(2 * hop) if j not in (hop - 1, hop)] + [hop - 1, hop]:
-            remote(ubuf.at[0], cbuf.at[i], c1s.at[0], c1r.at[i], y * nz + (z + 1) % nz, c).wait_recv()
-        total = ubuf[rr].astype(F32)
-        for k in range(2 * hop):
-            total = total + cbuf[k].astype(F32)
-        for b in range(nb + 1):
-            csrc[pl.ds(b, nc, stride=8), :] = total[:, b * LANES:(b + 1) * LANES]
-        csrc[pl.ds(nb + 1, nc, stride=8), :] = jnp.zeros((nc, LANES), F32)
-        for ch in range(nc):
-            is_own = jnp.logical_and(src_row == t, ch == c)
-
-            @pl.when(jnp.logical_not(is_own))
-            def _():
-                c2_copy(ch).start()
-
-            @pl.when(is_own)
-            def _():
-                block8(dbuf, slot_out)[...] = csrc[8 * ch:8 * ch + 8, :]
-
-    for yy in range(ny):
-        @pl.when(jnp.logical_or(yy != y, band != c))
-        def _():
-            remote(block8(csrc, 0), block8(dbuf, yy), c2s.at[0], c2r.at[yy], yy * nz + z, band).wait_recv()
-
-        @pl.when(jnp.logical_and(edge, jnp.logical_or(yy != y, edge_band != c)))
-        def _():
-            remote(
-                block8(csrc, 0), block8(dbuf, ny + yy), c2s.at[0], c2r.at[ny + yy], yy * nz + z, edge_band
-            ).wait_recv()
-    got = dbuf[0:8, :]
-    for k in range(1, 2 * ny):
-        got = got + dbuf[8 * k:8 * k + 8, :]
-    tail = got[nb:nb + 1, :]
+        ebuf[odd, y] = esrc[c]
+
+    for o in range(2):
+        for yy in range(ny):
+            cm = 2 * y + o
+            ce = feeders[2 + o]
+
+            @pl.when(jnp.logical_or(yy != y, cm != c))
+            def _():
+                remote(xsrc.at[0], mbuf.at[o, yy], xms.at[0], xmr.at[o, yy], yy * nz + z, cm).wait_recv()
+
+            @pl.when(jnp.logical_or(yy != y, ce != c))
+            def _():
+                remote(esrc.at[0], ebuf.at[o, yy], xes.at[0], xer.at[o, yy], yy * nz + z, ce).wait_recv()
+    rest = []
+    for o in range(2):
+        part = mbuf[o, 0].astype(F32)
+        side = ebuf[o, 0].astype(F32)
+        for yy in range(1, ny):
+            part = part + mbuf[o, yy].astype(F32)
+            side = side + ebuf[o, yy].astype(F32)
+        for b in range(nb):
+            zf[pl.ds(8 * rb * o + b, rb, stride=8), :] = part[b * rb:(b + 1) * rb, :]
+        tile = part[nb * rb:, :]
+        merged = jnp.where(kind8 == 1, tile + pltpu.roll(tile, LANES - PER, 1), tile)
+        merged = jnp.where(kind8 == 2, pltpu.roll(merged, PER, 1), merged)
+        count_row = halves(merged)[nb:nb + 1, :]
+        zf[pl.ds(8 * rb * o + nb, rb, stride=8), :] = jnp.broadcast_to(count_row, (rb, LANES))
+        zf[pl.ds(8 * rb * o + nb + 1, rb, stride=8), :] = jnp.zeros((rb, LANES), F32)
+        rest.append((jnp.where(row8 < nb, tile, 0.0), side))
+    extra = {rb: rest[0][0], rb - 1: rest[1][0], nz - 1: rest[0][1], 0: rest[1][1]}
+    for k in range(nz):
+        tile = zf[8 * k:8 * k + 8, :]
+        if k in extra:
+            tile = tile + extra[k]
+        zsrc[k] = tile.astype(BF)
+    around = [nz // 2] + [s * k for k in range(nz // 2 - 1, 0, -1) for s in (1, -1)]
+
+    def to_planes(f):
+        for d in around:
+            zt = (z + d + nz) % nz
+            f(remote(zsrc.at[zt], zbuf.at[z], zss.at[d % nz], zrs.at[z], y * nz + zt, c))
+
+    to_planes(lambda cp: cp.start())
+    zbuf[z] = zsrc[z]
+
+    for d in range(1, nz):
+        zt = (z + d) % nz
+        remote(zsrc.at[0], zbuf.at[zt], zss.at[0], zrs.at[zt], y * nz + zt, c).wait_recv()
+    got = zbuf[0].astype(F32)
+    for k in range(1, nz):
+        got = got + zbuf[k].astype(F32)
+    tail = pltpu.roll(got, (LANES - 16 * (z % rb)) % LANES, 1)[nb:nb + 1, :]
     number = jnp.zeros((1, LANES), F32)
     weight = jnp.zeros((1, LANES), F32)
     for u in range(PER):
@@ -465,18 +465,8 @@
     def _():
         for d in range(1, nz):
             remote(tbuf.at[rr], tbuf.at[rr], a2s.at[d], a2r.at[rr], y * nz + (z + d) % nz, c).wait_send()
-        for ch in range(nc):
-            @pl.when(jnp.logical_or(src_row != t, ch != c))
-            def _():
-                c2_copy(ch).wait_send()
-    to_relay(lambda cp: cp.wait_send())
-    to_gatherer(lambda cp: cp.wait_send())
-    for dist, lo, hi in relays:
-        k, out = relay_copy(dist)
-
-        @pl.when(k < nrow)
-        def _():
-            out.wait_send()
+    to_owners(lambda cp: cp.wait_send())
+    to_planes(lambda cp: cp.wait_send())
 
 
 def shards_fn(nt, nz, nc, data, basis, templates, spike_offset, spike_unit, spike_amp, seg_count, neighbors):
@@ -509,7 +499,6 @@
             pltpu.VMEM((1, slots), F32),
             pltpu.VMEM((1, 1), I32),
             pltpu.VMEM((8, neighbors.shape[0]), I32),
-            pltpu.VMEM(data.shape, BF),
             pltpu.VMEM((8, 2 * LANES), F32),
             pltpu.VMEM((8, LANES), F32),
             pltpu.VMEM((2, 8, LANES), F32),
@@ -524,17 +513,21 @@
             pltpu.VMEM((group, width), BF),
             pltpu.VMEM((group, 2 * LANES), BF),
             pltpu.VMEM((nrow, nc, width), BF),
-            pltpu.VMEM((nrow, nc, width + LANES), BF),
-            pltpu.VMEM((2 * hop - 1, nc, width + LANES), BF),
-            pltpu.VMEM((2 * hop, nc, width + LANES), BF),
-            pltpu.VMEM((8 * nc, LANES), F32),
-            pltpu.VMEM((16 * ny, LANES), F32),
+            pltpu.VMEM((nb, nrow * nc, LANES), F32),
+            pltpu.VMEM((2, 8 * nc, LANES), F32),
+            pltpu.VMEM((nc, nb * rb + 8, LANES), BF),
+            pltpu.VMEM((nc, 8, LANES), BF),
+            pltpu.VMEM((2, ny, nb * rb + 8, LANES), BF),
+            pltpu.VMEM((2, ny, 8, LANES), BF),
+            pltpu.VMEM((8 * nz, LANES), F32),
+            pltpu.VMEM((nz, 8, LANES), BF),
+            pltpu.VMEM((nz, 8, LANES), BF),
             dma((9,)), pltpu.SemaphoreType.REGULAR,
             dma((2,)), dma((2,)), dma((2,)), dma((2,)),
             dma((2 * ny,)), dma((nc,)),
             dma((nz,)), dma((nrow,)),
-            dma((nrow,)), dma((2 * hop,)), dma((2 * hop - 1,)),
-            dma((nc,)), dma((2 * ny,)),
+            dma((nc,)), dma((2, ny)), dma((nc,)), dma((2, ny)),
+            dma((nz,)), dma((nz,)),
         ],
         compiler_params=pltpu.CompilerParams(collective_id=0, has_side_effects=True),
         name="step",

time: 48.8 us -> 45.8 us (0.939)
  Pallas kernels: 46.1 us -> 43.1 us
    pallas_call x1, Pallas kernels: 46.1 us -> 43.1 us  [shards_fn(): pl.pallas_call(functools.partial(kernel, nt, nz, nc, group, taps), out_sh...]
where the time goes in v4:
time: 45.8 us; the launch traced here: 45.7 us
  Pallas kernels  43.1 us (94%)
  between operations  1.29 us (3%)
  local copies, waits for them, and re-layouts  1.27 us (3%)
    pallas_call x1, Pallas kernels, shards_fn(): pl.pallas_call(functools.partial(kernel, nt, nz, nc, group, taps), out_sh...  43.1 us
    unnamed x2, local copies, waits for them, and re-layouts  1.27 us

profile of v4, /device:TPU:1, one launch (start us, length us, event | category | flops | bytes accessed | tf_op | source)
XLA Modules:
  0.0 45.7 jit_solution(15484996945929894895)
XLA Ops:
  1.3 43.1 %step.1 = (bf16[768,128]{1,0:T(8,128)(2,1)S(1)}, f32[4,192]{1,0:T(4,128)S(1)}) custom-call(bf16[768,128]{1,0:T(8,128)(2,1)} %data_h.1, f32[6,61]{1,0:T(8,128)} %basis_h.1, f32[4,192]{1,0:T(4,128)} %templ_h.1, s32[1,32]{1,0:T(1,128)} %bitcast.7, s32[1,32]{1,0:T(1,128)} %bitcast.8, f32[1,32]{1,0:T(1,128)} %bitcast.9, s32[1,1]{1,0:T(1,128)} %bitcast.5.count_h, ...), custom_call_target="tpu_custom_call" | custom-call | tf_op jit(solution)/shard_map/step/pallas_call | solution.py:485
  44.4 0.7 %copy.12 = bf16[768,128]{1,0:T(8,128)(2,1)} copy(bf16[768,128]{1,0:T(8,128)(2,1)S(1)} %get-tuple-element.2) | data formatting | bytes 393216
  45.1 0.6 %copy.13 = f32[4,192]{1,0:T(4,128)} copy(f32[4,192]{1,0:T(4,128)S(1)} %get-tuple-element.3) | data formatting | bytes 6144
